TPU v7x, 32 devices: a whole 2x2x4 slice. The times are simulated.
32 devices in a mesh: fluid: 16 (over z, x, core), solid: 2 (over y).
Axes of the slice: x: 2, y: 2, z: 4, core: 2. Of those that a mesh axis runs over, the one named last changes fastest.
Arguments:
- fluid_load: float32 [2048, 3, 128], P(('fluid', 'solid')), may hold values from -6 to 6
- stiffness: float32 [2048, 3, 128], P(('fluid', 'solid')), may hold values from 0.2 to 2
- mapping: bfloat16 [2048, 128, 128], P(('fluid', 'solid')), may hold values from -0.5 to 0.5
- live_count: int32 [32], P(('fluid', 'solid')), may hold values from 40 to 64, as said below
- dest_device: int32 [2048, 1], P(('fluid', 'solid')), may hold values from 0 to 15; in each aligned block of 64 rows (0 to 63, 64 to 127, ...) at most 8 rows name the same one
- local_block: int32 [2048], P(('fluid', 'solid')), may hold values from 0 to 3
- compliance: float32 [2, 64, 3, 128], P('solid', 'fluid'), may hold values from 0.05 to 0.5
- start_disp: float32 [2, 64, 3, 128], P('solid', 'fluid'), may hold values from -40 to 40
- residual_history: float32 [50, 2, 64, 3, 128], P(None, 'solid', 'fluid'), may hold values from -40 to 40
- update_history: float32 [50, 2, 64, 3, 128], P(None, 'solid', 'fluid'), may hold values from -2.4 to 2.4
Outputs:
- displacement: float32 [2, 64, 3, 128], P('solid', 'fluid')
- fluid_displacement: float32 [2048, 3, 128], P(('fluid', 'solid'))
Inputs may be any that keep to these rules, and one draw needn't show every extreme that they name: `live_count`: each device's live blocks are its first ones; some device has exactly 64. `dest_device`: among the 64 rows of one device no fluid index appears more than 8 times.
All inputs are finite; a program needn't handle non-finite values.
Results may differ from a plain program's by a relative error of at most 0.0094.
Values may be sent and summed in bfloat16 or wider, within the bound.
A program may use at most 64 MiB of HBM per device.

v0:
```python
import jax
import jax.numpy as jnp
from jax import lax
from jax.sharding import PartitionSpec as P

ITERS = 2
ridge_share = 0.01


def solve_small(gram_matrix, right_side):
    order = gram_matrix.shape[0]
    ridge = ridge_share * jnp.trace(gram_matrix) / order
    factor = jnp.linalg.cholesky(gram_matrix + ridge * jnp.eye(order, dtype=gram_matrix.dtype))
    halfway = lax.linalg.triangular_solve(factor, right_side[:, None], left_side=True, lower=True)
    solved = lax.linalg.triangular_solve(
        factor, halfway, left_side=True, lower=True, transpose_a=True
    )
    return -solved[:, 0]


def full_sums(basis_flat, resid_flat):
    gram_local = jnp.dot(basis_flat, basis_flat.T, precision=lax.Precision.HIGHEST)
    right_local = jnp.dot(basis_flat, resid_flat, precision=lax.Precision.HIGHEST)
    return lax.psum((gram_local, right_local), ("fluid", "solid"))


def body(
    fluid_load,
    stiffness,
    mapping,
    live_count,
    dest_device,
    local_block,
    compliance,
    start_disp,
    residual_history,
    update_history,
):
    blocks = mapping.shape[0]
    struct_width = mapping.shape[1]
    sub_blocks = compliance.shape[1]
    fluid_size = lax.axis_size("fluid")
    alive = (jnp.arange(blocks) < live_count[0]).astype(jnp.float32)[:, None, None]
    capacity = max(2, 2 * ((blocks + fluid_size - 1) // fluid_size))
    dest_hot = (dest_device[:, 0][:, None] == jnp.arange(fluid_size)[None, :]).astype(jnp.int32)
    slot_rank = jnp.sum((jnp.cumsum(dest_hot, axis=0) - 1) * dest_hot, axis=1)
    slot_index = dest_device[:, 0] * capacity + slot_rank
    slot_hot = jnp.arange(fluid_size * capacity)[:, None] == slot_index[None, :]
    sent_ids = jnp.sum(slot_hot.astype(jnp.int32) * (local_block + 1)[None, :], axis=1) - 1
    owner_ids = lax.all_to_all(
        sent_ids.reshape(fluid_size, capacity), "fluid", split_axis=0, concat_axis=0, tiled=True
    )
    owner_hot = owner_ids.reshape(-1)[None, :] == jnp.arange(sub_blocks)[:, None]

    def to_fluid(struct_disp):
        packed = struct_disp[0].astype(jnp.bfloat16)
        chosen = jnp.einsum(
            "ks,kcj->scj",
            owner_hot.astype(jnp.bfloat16),
            packed,
            preferred_element_type=jnp.float32,
        ).astype(jnp.bfloat16)
        returned = lax.all_to_all(
            chosen.reshape(fluid_size, capacity, 3, struct_width),
            "fluid",
            split_axis=0,
            concat_axis=0,
            tiled=True,
        )
        picked = jnp.einsum(
            "sb,scj->bcj",
            slot_hot.astype(jnp.bfloat16),
            returned.reshape(-1, 3, struct_width),
            preferred_element_type=jnp.float32,
        )
        fluid_disp = jnp.einsum(
            "bjn,bcj->bcn", mapping, picked.astype(jnp.bfloat16), preferred_element_type=jnp.float32
        )
        return fluid_disp * alive

    struct_disp = start_disp
    basis_cols = residual_history
    updates = update_history
    last_resid = struct_disp
    last_image = struct_disp
    gram_matrix = None
    for iteration in range(ITERS):
        fluid_disp = to_fluid(struct_disp)
        fluid_force = (alive * (fluid_load - stiffness * fluid_disp)).astype(jnp.bfloat16)
        contrib = jnp.einsum(
            "bjn,bcn->bcj", mapping, fluid_force, preferred_element_type=jnp.float32
        )
        buffer = jnp.einsum(
            "sb,bcj->scj", slot_hot.astype(jnp.float32), contrib, precision=lax.Precision.HIGHEST
        )
        received = lax.all_to_all(
            buffer.reshape(fluid_size, capacity, 3, struct_width),
            "fluid",
            split_axis=0,
            concat_axis=0,
            tiled=True,
        )
        summed = jnp.einsum(
            "ks,scj->kcj",
            owner_hot.astype(jnp.float32),
            received.reshape(-1, 3, struct_width),
            precision=lax.Precision.HIGHEST,
        )
        struct_image = compliance * summed[None]
        residual = struct_image - struct_disp
        newest = residual - last_resid
        if iteration > 0:
            basis_cols = jnp.concatenate([basis_cols[1:], newest[None]], 0)
            updates = jnp.concatenate([updates[1:], (struct_image - last_image)[None]], 0)
        basis_flat = basis_cols.reshape(basis_cols.shape[0], -1)
        resid_flat = residual.reshape(-1)
        gram_matrix, right_side = full_sums(basis_flat, resid_flat)
        coefficients = solve_small(gram_matrix, right_side)
        struct_disp = struct_image + jnp.tensordot(
            coefficients, updates, axes=1, precision=lax.Precision.HIGHEST
        )
        last_resid = residual
        last_image = struct_image
    final_disp = to_fluid(struct_disp)
    return (struct_disp, final_disp)


def solution(mesh):
    in_specs = (
        P(("fluid", "solid"), None, None),
        P(("fluid", "solid"), None, None),
        P(("fluid", "solid"), None, None),
        P(("fluid", "solid")),
        P(("fluid", "solid"), None),
        P(("fluid", "solid")),
        P("solid", "fluid", None, None),
        P("solid", "fluid", None, None),
        P(None, "solid", "fluid", None, None),
        P(None, "solid", "fluid", None, None),
    )
    out_specs = (P("solid", "fluid", None, None), P(("fluid", "solid"), None, None))
    return jax.shard_map(body, mesh=mesh, in_specs=in_specs, out_specs=out_specs, check_vma=False)
```

profile of v0, /device:TPU:0, one launch (start us, length us, event | category | flops | bytes accessed | tf_op | source)
XLA Modules:
  0.0 190.6 jit_solution(16942165006575213732)
XLA Ops:
  0.6 0.0 copy-start
  0.6 0.9 fusion.48
  1.5 0.1 reduce_window_sum.11
  1.6 0.8 select_reduce_fusion.1
  2.5 0.7 multiply_add_fusion
  3.1 0.1 select_reduce_fusion
  3.2 0.1 sub.30
  3.3 13.6 %all_to_all.31 = s32[16,1,8]{2,1,0:T(1,128)S(1)} all-to-all(s32[16,1,8]{2,1,0:T(1,128)S(1)} %bitcast.179), channel_id=1, replica_groups=mesh['fluid'=16,'solid'=2] {'fluid'}, dimensions={0} | all-to-all | bytes 1024 | tf_op jit(solution)/shard_map/all_to_all | solution.py:50
  17.0 0.5 broadcast.90
  17.5 0.7 reduce.7
  18.1 0.1 eq.60
  18.2 0.9 fusion.8
  19.2 0.7 copy.39
  19.8 3.5 %all-to-all-start.1 = ((bf16[16,8,3,128]{3,1,2,0:T(8,128)(2,1)}), bf16[16,8,3,128]{3,1,2,0:T(8,128)(2,1)S(1)}, u32[]{:S(2)}, u32[]{:S(2)}) async-start(bf16[16,8,3,128]{3,1,2,0:T(8,128)(2,1)} %copy.39), calls=%async_computation.1 | async-start | bytes 196608 | tf_op jit(solution)/shard_map/all_to_all | solution.py:63
  24.0 6.7 %all-to-all-done.1 = bf16[16,8,3,128]{3,1,2,0:T(8,128)(2,1)S(1)} async-done(((bf16[16,8,3,128]{3,1,2,0:T(8,128)(2,1)}), bf16[16,8,3,128]{3,1,2,0:T(8,128)(2,1)S(1)}, u32[]{:S(2)}, u32[]{:S(2)}) %all-to-all-start.1) | async-done | bytes 98336 | tf_op jit(solution)/shard_map/all_to_all | solution.py:63
  30.7 0.2 convolution_convert_fusion.5
  30.9 0.0 copy-start.1
  30.9 0.0 copy-start.5
  30.9 0.0 copy-start.6
  30.9 2.7 %fusion.12 = f32[64,3,128]{2,1,0:T(4,128)S(1)} fusion(bf16[64,128,128]{2,1,0:T(8,128)(2,1)S(1)} %copy-done, f32[64,3,128]{2,0,1:T(8,128)} %param.15, f32[64,3,128]{2,0,1:T(8,128)} %param.16, bf16[64,3,128]{2,0,1:T(8,128)(2,1)S(1)} %convolution_convert_fusion.5, f32[64]{0:T(128)S(1)} %compare_convert_fusion), kind=kOutput, calls=%fused_computation.23 | convolution fusion | flops 12705792 | bytes 2441472 | tf_op jit(solution)/shard_map/bjn,bcn->bcj/dot_general | solution.py:90
  33.7 0.4 convolution_bitcast_fusion.1
  34.0 0.7 copy.45
  34.7 3.5 %all-to-all-start.2 = ((f32[16,8,3,128]{3,1,2,0:T(8,128)}), f32[16,8,3,128]{3,1,2,0:T(8,128)S(1)}, u32[]{:S(2)}, u32[]{:S(2)}) async-start(f32[16,8,3,128]{3,1,2,0:T(8,128)} %copy.45), calls=%async_computation.2 | async-start | bytes 393216 | tf_op jit(solution)/shard_map/all_to_all | solution.py:96
  38.3 0.4 convolution_bitcast_fusion.3
  38.7 8.5 %all-to-all-done.2 = f32[16,8,3,128]{3,1,2,0:T(8,128)S(1)} async-done(((f32[16,8,3,128]{3,1,2,0:T(8,128)}), f32[16,8,3,128]{3,1,2,0:T(8,128)S(1)}, u32[]{:S(2)}, u32[]{:S(2)}) %all-to-all-start.2) | async-done | bytes 196640 | tf_op jit(solution)/shard_map/all_to_all | solution.py:96
  47.2 0.2 fusion.84
  47.4 0.4 convolution_bitcast_fusion.7
  47.7 37.9 %all-reduce.1 = (f32[50,1]{0,1:T(1,128)S(1)}, f32[50,50]{0,1:T(8,128)S(1)}) all-reduce(f32[50,1]{0,1:T(1,128)S(1)} %convolution_bitcast_fusion.7, f32[50,50]{0,1:T(8,128)S(1)} %convolution_bitcast_fusion.3), channel_id=1, replica_groups=mesh['fluid'=16,'solid'=2] {'fluid','solid'}, use_global_device_ids=true, to_apply=%region_7.9 | all-reduce | flops 2550 | bytes 20400 | tf_op jit(solution)/shard_map/psum | solution.py:24
  85.6 0.6 select_reduce_fusion.5
  86.9 0.1 copy.50
  87.0 4.6 %cholesky.44 = f32[50,50]{1,0:T(8,128)S(1)} custom-call(f32[50,50]{1,0:T(8,128)S(1)} %fusion.62), custom_call_target="Cholesky" | custom-call | tf_op jit(solution)/shard_map/jit(cholesky)/cholesky | solution.py:13
  91.6 0.6 compare_reduce_fusion.1
  92.3 0.7 fusion.55
  92.9 3.8 %custom-call.11 = f32[1,50,50]{1,2,0:T(8,128)S(1)} custom-call(f32[1,50,50]{2,1,0:T(8,128)S(1)} %fusion.55), custom_call_target="InvertDiagBlocksLowerTriangular" | custom-call | tf_op jit(solution)/shard_map/triangular_solve/custom-call.2 | solution.py:15
  96.8 0.2 convolution_bitcast_fusion.11
  96.9 0.2 fusion.18
  97.1 0.3 fusion.21
  97.4 0.3 fusion.9
  97.7 12.5 %all_to_all.32 = bf16[16,8,3,128]{3,1,2,0:T(8,128)(2,1)S(1)} all-to-all(bf16[16,8,3,128]{3,1,2,0:T(8,128)(2,1)S(1)} %copy.51), channel_id=1, replica_groups=mesh['fluid'=16,'solid'=2] {'fluid'}, dimensions={0} | all-to-all | bytes 196608 | tf_op jit(solution)/shard_map/all_to_all | solution.py:63
  110.1 0.2 convolution_convert_fusion.4
  110.4 1.7 fusion.11
  112.1 0.4 convolution_bitcast_fusion
  112.5 0.7 copy.57
  113.2 3.5 %all-to-all-start.4 = ((f32[16,8,3,128]{3,1,2,0:T(8,128)}), f32[16,8,3,128]{3,1,2,0:T(8,128)S(1)}, u32[]{:S(2)}, u32[]{:S(2)}) async-start(f32[16,8,3,128]{3,1,2,0:T(8,128)} %copy.57), calls=%async_computation.4 | async-start | bytes 393216 | tf_op jit(solution)/shard_map/all_to_all | solution.py:96
  116.8 8.8 %all-to-all-done.4 = f32[16,8,3,128]{3,1,2,0:T(8,128)S(1)} async-done(((f32[16,8,3,128]{3,1,2,0:T(8,128)}), f32[16,8,3,128]{3,1,2,0:T(8,128)S(1)}, u32[]{:S(2)}, u32[]{:S(2)}) %all-to-all-start.4) | async-done | bytes 196640 | tf_op jit(solution)/shard_map/all_to_all | solution.py:96
  125.6 0.2 fusion.13
  125.8 0.4 convolution_bitcast_fusion.2
  126.3 0.4 convolution_bitcast_fusion.6
  126.6 37.9 %all-reduce = (f32[50,1]{0,1:T(1,128)S(1)}, f32[50,50]{0,1:T(8,128)S(1)}) all-reduce(f32[50,1]{0,1:T(1,128)S(1)} %convolution_bitcast_fusion.6, f32[50,50]{0,1:T(8,128)S(1)} %convolution_bitcast_fusion.2), channel_id=1, replica_groups=mesh['fluid'=16,'solid'=2] {'fluid','solid'}, use_global_device_ids=true, to_apply=%region_10.14 | all-reduce | flops 2550 | bytes 20400 | tf_op jit(solution)/shard_map/psum | solution.py:24
  164.5 0.6 select_reduce_fusion.4
  165.8 0.1 copy.62
  165.9 4.6 %cholesky.55 = f32[50,50]{1,0:T(8,128)S(1)} custom-call(f32[50,50]{1,0:T(8,128)S(1)} %fusion.59), custom_call_target="Cholesky" | custom-call | tf_op jit(solution)/shard_map/jit(cholesky)/cholesky | solution.py:13
  170.5 0.6 compare_reduce_fusion
  171.2 0.7 fusion.56
  171.8 3.8 %custom-call.13 = f32[1,50,50]{1,2,0:T(8,128)S(1)} custom-call(f32[1,50,50]{2,1,0:T(8,128)S(1)} %fusion.56), custom_call_target="InvertDiagBlocksLowerTriangular" | custom-call | tf_op jit(solution)/shard_map/triangular_solve/custom-call.2 | solution.py:15
  175.6 0.2 convolution_bitcast_fusion.9
  175.8 0.2 fusion.16
  176.0 0.1 maximum_bitcast_fusion.1
  176.0 0.3 fusion.19
  176.4 0.3 fusion.10
  176.6 12.5 %all_to_all.33 = bf16[16,8,3,128]{3,1,2,0:T(8,128)(2,1)S(1)} all-to-all(bf16[16,8,3,128]{3,1,2,0:T(8,128)(2,1)S(1)} %copy.63), channel_id=1, replica_groups=mesh['fluid'=16,'solid'=2] {'fluid'}, dimensions={0} | all-to-all | bytes 196608 | tf_op jit(solution)/shard_map/all_to_all | solution.py:63
  189.1 0.2 convolution_convert_fusion.3
  189.3 0.6 convolution_multiply_fusion
  190.0 0.7 copy.66
  (28 shorter events, 0.3 us)
Async XLA Ops:
  0.6 30.3 %copy-start = (bf16[64,128,128]{2,1,0:T(8,128)(2,1)S(1)}, bf16[64,128,128]{2,1,0:T(8,128)(2,1)}, u32[]{:S(2)}) copy-start(bf16[64,128,128]{2,1,0:T(8,128)(2,1)} %param.17) | copy-start | bytes 6291460
  19.8 10.9 %all-to-all-start.1 = ((bf16[16,8,3,128]{3,1,2,0:T(8,128)(2,1)}), bf16[16,8,3,128]{3,1,2,0:T(8,128)(2,1)S(1)}, u32[]{:S(2)}, u32[]{:S(2)}) async-start(bf16[16,8,3,128]{3,1,2,0:T(8,128)(2,1)} %copy.39), calls=%async_computation.1 | async-start | bytes 196608 | tf_op jit(solution)/shard_map/all_to_all | solution.py:63
  30.9 7.3 %copy-start.1 = (f32[50,1,4,3,128]{4,2,3,1,0:T(4,128)S(1)}, f32[50,1,4,3,128]{4,2,3,1,0:T(4,128)}, u32[]{:S(2)}) copy-start(f32[50,1,4,3,128]{4,2,3,1,0:T(4,128)} %param.23) | copy-start | bytes 921604
  30.9 16.3 %copy-start.5 = (f32[1,4,3,128]{3,1,2,0:T(4,128)S(1)}, f32[1,4,3,128]{3,1,2,0:T(4,128)}, u32[]{:S(2)}) copy-start(f32[1,4,3,128]{3,1,2,0:T(4,128)} %param.21) | copy-start | bytes 18436
  30.9 16.3 %copy-start.6 = (f32[1,4,3,128]{3,1,2,0:T(4,128)S(1)}, f32[1,4,3,128]{3,1,2,0:T(4,128)}, u32[]{:S(2)}) copy-start(f32[1,4,3,128]{3,1,2,0:T(4,128)} %param.22) | copy-start | bytes 18436
  33.6 63.4 %copy-start.2 = (f32[50,1,4,3,128]{4,2,3,1,0:T(4,128)S(1)}, f32[50,1,4,3,128]{4,2,3,1,0:T(4,128)}, u32[]{:S(2)}) copy-start(f32[50,1,4,3,128]{4,2,3,1,0:T(4,128)} %param.24) | copy-start | bytes 921604
  33.6 76.7 %copy-start.3 = (f32[64,3,128]{2,0,1:T(8,128)S(1)}, f32[64,3,128]{2,0,1:T(8,128)}, u32[]{:S(2)}) copy-start(f32[64,3,128]{2,0,1:T(8,128)} %param.15) | copy-start | bytes 294916
  33.6 76.7 %copy-start.4 = (f32[64,3,128]{2,0,1:T(8,128)S(1)}, f32[64,3,128]{2,0,1:T(8,128)}, u32[]{:S(2)}) copy-start(f32[64,3,128]{2,0,1:T(8,128)} %param.16) | copy-start | bytes 294916
  34.7 12.5 %all-to-all-start.2 = ((f32[16,8,3,128]{3,1,2,0:T(8,128)}), f32[16,8,3,128]{3,1,2,0:T(8,128)S(1)}, u32[]{:S(2)}, u32[]{:S(2)}) async-start(f32[16,8,3,128]{3,1,2,0:T(8,128)} %copy.45), calls=%async_computation.2 | async-start | bytes 393216 | tf_op jit(solution)/shard_map/all_to_all | solution.py:96
  113.2 12.5 %all-to-all-start.4 = ((f32[16,8,3,128]{3,1,2,0:T(8,128)}), f32[16,8,3,128]{3,1,2,0:T(8,128)S(1)}, u32[]{:S(2)}, u32[]{:S(2)}) async-start(f32[16,8,3,128]{3,1,2,0:T(8,128)} %copy.57), calls=%async_computation.4 | async-start | bytes 393216 | tf_op jit(solution)/shard_map/all_to_all | solution.py:96
  176.3 14.3 %copy-start.7 = (f32[1,4,3,128]{3,1,2,0:T(4,128)}, f32[1,4,3,128]{3,1,2,0:T(4,128)S(1)}, u32[]{:S(2)}) copy-start(f32[1,4,3,128]{3,1,2,0:T(4,128)S(1)} %copy_add_fusion) | copy-start | bytes 18436
where the time goes:
time: 192 us; the launch traced here: 191 us
  blocking collectives  114 us (59%)
  other arithmetic  24.1 us (13%)
  waiting for transfers between devices  24 us (12%)
  matrix products  11 us (6%)
  starting transfers between devices  10.5 us (5%)
  local copies, waits for them, and re-layouts  3.73 us (2%)
  between operations  2.92 us (2%)
    psum x2, blocking collectives, full_sums(): return lax.psum((gram_local, right_local), ('fluid', 'solid'))  75.8 us
    all_to_all x2, blocking collectives, to_fluid(): lax.all_to_all(chosen.reshape(fluid_size, capacity, 3, struct_width), 'fl...  24.9 us
    all_to_all x2, waiting for transfers between devices, body(): lax.all_to_all(buffer.reshape(fluid_size, capacity, 3, struct_width), 'fl...  17.3 us
    all_to_all x1, blocking collectives, body(): lax.all_to_all(sent_ids.reshape(fluid_size, capacity), 'fluid', split_axi...  13.6 us
    another operation x6, other arithmetic, solve_small(): jnp.linalg.cholesky(gram_matrix + ridge * jnp.eye(order, dtype=gram_matri...  10.5 us
    another operation x4, other arithmetic, solve_small(): lax.linalg.triangular_solve(factor, halfway, left_side=True, lower=True,...  8.96 us
    all_to_all x2, starting transfers between devices, body(): lax.all_to_all(buffer.reshape(fluid_size, capacity, 3, struct_width), 'fl...  7.04 us
    all_to_all x1, waiting for transfers between devices, to_fluid(): lax.all_to_all(chosen.reshape(fluid_size, capacity, 3, struct_width), 'fl...  6.69 us
  transfers between devices with their start and end apart: 3, of which 3 were waited for; matrix products, arithmetic and copies ran while one was open for 0% of the time, Pallas kernels for 0%

commit v1 on v0

--- a/solution.py
+++ b/solution.py
@@ -21,7 +21,7 @@
 def full_sums(basis_flat, resid_flat):
     gram_local = jnp.dot(basis_flat, basis_flat.T, precision=lax.Precision.HIGHEST)
     right_local = jnp.dot(basis_flat, resid_flat, precision=lax.Precision.HIGHEST)
-    return lax.psum((gram_local, right_local), ("fluid", "solid"))
+    return lax.psum(lax.psum((gram_local, right_local), "solid"), "fluid")
 
 
 def body(

time: 192 us -> 242 us (1.26)
  blocking collectives: 114 us -> 165 us
    psum x2 -> x4, blocking collectives: 75.8 us -> 131 us  [full_sums(): return lax.psum(lax.psum((gram_local, right_local), 'solid'), 'fluid')]
    all_to_all x2, blocking collectives: 24.9 us -> 19.9 us  [to_fluid(): lax.all_to_all(chosen.reshape(fluid_size, capacity, 3, struct_width), 'fl...]
where the time goes in v1:
time: 242 us; the launch traced here: 241 us
  blocking collectives  165 us (68%)
  other arithmetic  24.1 us (10%)
  waiting for transfers between devices  24 us (10%)
  matrix products  11 us (5%)
  starting transfers between devices  10.5 us (4%)
  local copies, waits for them, and re-layouts  3.73 us (2%)
  between operations  2.91 us (1%)
    psum x4, blocking collectives, full_sums(): return lax.psum(lax.psum((gram_local, right_local), 'solid'), 'fluid')  131 us
    all_to_all x2, blocking collectives, to_fluid(): lax.all_to_all(chosen.reshape(fluid_size, capacity, 3, struct_width), 'fl...  19.9 us
    all_to_all x2, waiting for transfers between devices, body(): lax.all_to_all(buffer.reshape(fluid_size, capacity, 3, struct_width), 'fl...  17.3 us
    all_to_all x1, blocking collectives, body(): lax.all_to_all(sent_ids.reshape(fluid_size, capacity), 'fluid', split_axi...  13.6 us
    another operation x6, other arithmetic, solve_small(): jnp.linalg.cholesky(gram_matrix + ridge * jnp.eye(order, dtype=gram_matri...  10.5 us
    another operation x4, other arithmetic, solve_small(): lax.linalg.triangular_solve(factor, halfway, left_side=True, lower=True,...  8.96 us
    all_to_all x2, starting transfers between devices, body(): lax.all_to_all(buffer.reshape(fluid_size, capacity, 3, struct_width), 'fl...  7.04 us
    all_to_all x1, waiting for transfers between devices, to_fluid(): lax.all_to_all(chosen.reshape(fluid_size, capacity, 3, struct_width), 'fl...  6.69 us
  transfers between devices with their start and end apart: 3, of which 3 were waited for; matrix products, arithmetic and copies ran while one was open for 0% of the time, Pallas kernels for 0%

profile of v1, /device:TPU:0, one launch (start us, length us, event | category | flops | bytes accessed | tf_op | source)
XLA Modules:
  0.0 240.9 jit_solution(5126716466400699133)
XLA Ops:
  0.6 0.0 copy-start
  0.6 0.9 fusion.48
  1.5 0.1 reduce_window_sum.11
  1.6 0.8 select_reduce_fusion.1
  2.5 0.7 multiply_add_fusion
  3.1 0.1 select_reduce_fusion
  3.2 0.1 sub.30
  3.3 13.6 %all_to_all.31 = s32[16,1,8]{2,1,0:T(1,128)S(1)} all-to-all(s32[16,1,8]{2,1,0:T(1,128)S(1)} %bitcast.177), channel_id=1, replica_groups=mesh['fluid'=16,'solid'=2] {'fluid'}, dimensions={0} | all-to-all | bytes 1024 | tf_op jit(solution)/shard_map/all_to_all | solution.py:50
  17.0 0.5 broadcast.90
  17.5 0.7 reduce.7
  18.1 0.1 eq.60
  18.2 0.9 fusion.8
  19.2 0.7 copy.39
  19.8 3.5 %all-to-all-start.1 = ((bf16[16,8,3,128]{3,1,2,0:T(8,128)(2,1)}), bf16[16,8,3,128]{3,1,2,0:T(8,128)(2,1)S(1)}, u32[]{:S(2)}, u32[]{:S(2)}) async-start(bf16[16,8,3,128]{3,1,2,0:T(8,128)(2,1)} %copy.39), calls=%async_computation.1 | async-start | bytes 196608 | tf_op jit(solution)/shard_map/all_to_all | solution.py:63
  24.0 6.7 %all-to-all-done.1 = bf16[16,8,3,128]{3,1,2,0:T(8,128)(2,1)S(1)} async-done(((bf16[16,8,3,128]{3,1,2,0:T(8,128)(2,1)}), bf16[16,8,3,128]{3,1,2,0:T(8,128)(2,1)S(1)}, u32[]{:S(2)}, u32[]{:S(2)}) %all-to-all-start.1) | async-done | bytes 98336 | tf_op jit(solution)/shard_map/all_to_all | solution.py:63
  30.7 0.2 convolution_convert_fusion.5
  30.9 0.0 copy-start.1
  30.9 2.7 %fusion.12 = f32[64,3,128]{2,1,0:T(4,128)S(1)} fusion(bf16[64,128,128]{2,1,0:T(8,128)(2,1)S(1)} %copy-done, f32[64,3,128]{2,0,1:T(8,128)} %param.15, f32[64,3,128]{2,0,1:T(8,128)} %param.16, bf16[64,3,128]{2,0,1:T(8,128)(2,1)S(1)} %convolution_convert_fusion.5, f32[64]{0:T(128)S(1)} %compare_convert_fusion), kind=kOutput, calls=%fused_computation.23 | convolution fusion | flops 12705792 | bytes 2441472 | tf_op jit(solution)/shard_map/bjn,bcn->bcj/dot_general | solution.py:90
  33.7 0.4 convolution_bitcast_fusion.1
  34.0 0.7 copy.45
  34.7 3.5 %all-to-all-start.2 = ((f32[16,8,3,128]{3,1,2,0:T(8,128)}), f32[16,8,3,128]{3,1,2,0:T(8,128)S(1)}, u32[]{:S(2)}, u32[]{:S(2)}) async-start(f32[16,8,3,128]{3,1,2,0:T(8,128)} %copy.45), calls=%async_computation.2 | async-start | bytes 393216 | tf_op jit(solution)/shard_map/all_to_all | solution.py:96
  38.3 0.4 convolution_bitcast_fusion.3
  38.7 8.5 %all-to-all-done.2 = f32[16,8,3,128]{3,1,2,0:T(8,128)S(1)} async-done(((f32[16,8,3,128]{3,1,2,0:T(8,128)}), f32[16,8,3,128]{3,1,2,0:T(8,128)S(1)}, u32[]{:S(2)}, u32[]{:S(2)}) %all-to-all-start.2) | async-done | bytes 196640 | tf_op jit(solution)/shard_map/all_to_all | solution.py:96
  47.2 0.2 fusion.84
  47.4 0.4 convolution_bitcast_fusion.7
  47.7 8.4 %all-reduce.3 = (f32[50]{0:T(128)S(1)}, f32[50,50]{0,1:T(8,128)S(1)}) all-reduce(f32[50]{0:T(128)S(1)} %convolution_bitcast_fusion.7, f32[50,50]{0,1:T(8,128)S(1)} %convolution_bitcast_fusion.3), channel_id=1, replica_groups=mesh['fluid'=16,'solid'=2] {'solid'}, use_global_device_ids=true, to_apply=%region_8.10 | all-reduce | flops 2550 | bytes 20400 | tf_op jit(solution)/shard_map/psum | solution.py:24
  56.1 57.7 %all-reduce.1 = (f32[50,1]{0,1:T(1,128)S(1)}, f32[50,50]{0,1:T(8,128)S(1)}) all-reduce(f32[50,1]{0,1:T(1,128)S(1)} %bitcast.180, f32[50,50]{0,1:T(8,128)S(1)} %get-tuple-element.18), channel_id=1, replica_groups=mesh['fluid'=16,'solid'=2] {'fluid'}, use_global_device_ids=true, to_apply=%region_9.11 | all-reduce | flops 2550 | bytes 20400 | tf_op jit(solution)/shard_map/psum | solution.py:24
  113.8 0.6 select_reduce_fusion.5
  115.1 0.1 copy.50
  115.2 4.6 %cholesky.44 = f32[50,50]{1,0:T(8,128)S(1)} custom-call(f32[50,50]{1,0:T(8,128)S(1)} %fusion.62), custom_call_target="Cholesky" | custom-call | tf_op jit(solution)/shard_map/jit(cholesky)/cholesky | solution.py:13
  119.8 0.6 compare_reduce_fusion.1
  120.4 0.7 fusion.55
  121.1 3.8 %custom-call.11 = f32[1,50,50]{1,2,0:T(8,128)S(1)} custom-call(f32[1,50,50]{2,1,0:T(8,128)S(1)} %fusion.55), custom_call_target="InvertDiagBlocksLowerTriangular" | custom-call | tf_op jit(solution)/shard_map/triangular_solve/custom-call.2 | solution.py:15
  124.9 0.2 convolution_bitcast_fusion.11
  125.1 0.2 fusion.18
  125.2 0.3 fusion.21
  125.6 0.3 fusion.9
  125.8 10.0 %all_to_all.32 = bf16[16,8,3,128]{3,1,2,0:T(8,128)(2,1)S(1)} all-to-all(bf16[16,8,3,128]{3,1,2,0:T(8,128)(2,1)S(1)} %copy.51), channel_id=1, replica_groups=mesh['fluid'=16,'solid'=2] {'fluid'}, dimensions={0} | all-to-all | bytes 196608 | tf_op jit(solution)/shard_map/all_to_all | solution.py:63
  135.8 0.2 convolution_convert_fusion.4
  136.0 1.7 fusion.11
  137.8 0.4 convolution_bitcast_fusion
  138.1 0.7 copy.57
  138.8 3.5 %all-to-all-start.4 = ((f32[16,8,3,128]{3,1,2,0:T(8,128)}), f32[16,8,3,128]{3,1,2,0:T(8,128)S(1)}, u32[]{:S(2)}, u32[]{:S(2)}) async-start(f32[16,8,3,128]{3,1,2,0:T(8,128)} %copy.57), calls=%async_computation.4 | async-start | bytes 393216 | tf_op jit(solution)/shard_map/all_to_all | solution.py:96
  142.5 8.8 %all-to-all-done.4 = f32[16,8,3,128]{3,1,2,0:T(8,128)S(1)} async-done(((f32[16,8,3,128]{3,1,2,0:T(8,128)}), f32[16,8,3,128]{3,1,2,0:T(8,128)S(1)}, u32[]{:S(2)}, u32[]{:S(2)}) %all-to-all-start.4) | async-done | bytes 196640 | tf_op jit(solution)/shard_map/all_to_all | solution.py:96
  151.3 0.2 fusion.13
  151.5 0.4 convolution_bitcast_fusion.2
  151.9 0.4 convolution_bitcast_fusion.6
  152.3 7.4 %all-reduce.2 = (f32[50]{0:T(128)S(1)}, f32[50,50]{0,1:T(8,128)S(1)}) all-reduce(f32[50]{0:T(128)S(1)} %convolution_bitcast_fusion.6, f32[50,50]{0,1:T(8,128)S(1)} %convolution_bitcast_fusion.2), channel_id=1, replica_groups=mesh['fluid'=16,'solid'=2] {'solid'}, use_global_device_ids=true, to_apply=%region_13.17 | all-reduce | flops 2550 | bytes 20400 | tf_op jit(solution)/shard_map/psum | solution.py:24
  159.7 57.7 %all-reduce = (f32[50,1]{0,1:T(1,128)S(1)}, f32[50,50]{0,1:T(8,128)S(1)}) all-reduce(f32[50,1]{0,1:T(1,128)S(1)} %bitcast.181, f32[50,50]{0,1:T(8,128)S(1)} %get-tuple-element.16), channel_id=1, replica_groups=mesh['fluid'=16,'solid'=2] {'fluid'}, use_global_device_ids=true, to_apply=%region_14.18 | all-reduce | flops 2550 | bytes 20400 | tf_op jit(solution)/shard_map/psum | solution.py:24
  217.3 0.6 select_reduce_fusion.4
  218.6 0.1 copy.62
  218.7 4.6 %cholesky.55 = f32[50,50]{1,0:T(8,128)S(1)} custom-call(f32[50,50]{1,0:T(8,128)S(1)} %fusion.59), custom_call_target="Cholesky" | custom-call | tf_op jit(solution)/shard_map/jit(cholesky)/cholesky | solution.py:13
  223.3 0.6 compare_reduce_fusion
  224.0 0.7 fusion.56
  224.6 3.8 %custom-call.13 = f32[1,50,50]{1,2,0:T(8,128)S(1)} custom-call(f32[1,50,50]{2,1,0:T(8,128)S(1)} %fusion.56), custom_call_target="InvertDiagBlocksLowerTriangular" | custom-call | tf_op jit(solution)/shard_map/triangular_solve/custom-call.2 | solution.py:15
  228.5 0.2 convolution_bitcast_fusion.9
  228.6 0.2 fusion.16
  228.8 0.1 maximum_bitcast_fusion.1
  228.9 0.3 fusion.19
  229.2 0.3 fusion.10
  229.5 10.0 %all_to_all.33 = bf16[16,8,3,128]{3,1,2,0:T(8,128)(2,1)S(1)} all-to-all(bf16[16,8,3,128]{3,1,2,0:T(8,128)(2,1)S(1)} %copy.63), channel_id=1, replica_groups=mesh['fluid'=16,'solid'=2] {'fluid'}, dimensions={0} | all-to-all | bytes 196608 | tf_op jit(solution)/shard_map/all_to_all | solution.py:63
  239.4 0.2 convolution_convert_fusion.3
  239.6 0.6 convolution_multiply_fusion
  240.3 0.7 copy.66
  (30 shorter events, 0.3 us)
Async XLA Ops:
  0.6 30.3 %copy-start = (bf16[64,128,128]{2,1,0:T(8,128)(2,1)S(1)}, bf16[64,128,128]{2,1,0:T(8,128)(2,1)}, u32[]{:S(2)}) copy-start(bf16[64,128,128]{2,1,0:T(8,128)(2,1)} %param.17) | copy-start | bytes 6291460
  19.8 10.9 %all-to-all-start.1 = ((bf16[16,8,3,128]{3,1,2,0:T(8,128)(2,1)}), bf16[16,8,3,128]{3,1,2,0:T(8,128)(2,1)S(1)}, u32[]{:S(2)}, u32[]{:S(2)}) async-start(bf16[16,8,3,128]{3,1,2,0:T(8,128)(2,1)} %copy.39), calls=%async_computation.1 | async-start | bytes 196608 | tf_op jit(solution)/shard_map/all_to_all | solution.py:63
  30.9 7.3 %copy-start.1 = (f32[50,1,4,3,128]{4,2,3,1,0:T(4,128)S(1)}, f32[50,1,4,3,128]{4,2,3,1,0:T(4,128)}, u32[]{:S(2)}) copy-start(f32[50,1,4,3,128]{4,2,3,1,0:T(4,128)} %param.23) | copy-start | bytes 921604
  30.9 16.3 %copy-start.5 = (f32[1,4,3,128]{3,1,2,0:T(4,128)S(1)}, f32[1,4,3,128]{3,1,2,0:T(4,128)}, u32[]{:S(2)}) copy-start(f32[1,4,3,128]{3,1,2,0:T(4,128)} %param.21) | copy-start | bytes 18436
  30.9 16.3 %copy-start.6 = (f32[1,4,3,128]{3,1,2,0:T(4,128)S(1)}, f32[1,4,3,128]{3,1,2,0:T(4,128)}, u32[]{:S(2)}) copy-start(f32[1,4,3,128]{3,1,2,0:T(4,128)} %param.22) | copy-start | bytes 18436
  33.6 91.6 %copy-start.2 = (f32[50,1,4,3,128]{4,2,3,1,0:T(4,128)S(1)}, f32[50,1,4,3,128]{4,2,3,1,0:T(4,128)}, u32[]{:S(2)}) copy-start(f32[50,1,4,3,128]{4,2,3,1,0:T(4,128)} %param.24) | copy-start | bytes 921604
  33.6 102.4 %copy-start.3 = (f32[64,3,128]{2,0,1:T(8,128)S(1)}, f32[64,3,128]{2,0,1:T(8,128)}, u32[]{:S(2)}) copy-start(f32[64,3,128]{2,0,1:T(8,128)} %param.15) | copy-start | bytes 294916
  33.6 102.4 %copy-start.4 = (f32[64,3,128]{2,0,1:T(8,128)S(1)}, f32[64,3,128]{2,0,1:T(8,128)}, u32[]{:S(2)}) copy-start(f32[64,3,128]{2,0,1:T(8,128)} %param.16) | copy-start | bytes 294916
  34.7 12.5 %all-to-all-start.2 = ((f32[16,8,3,128]{3,1,2,0:T(8,128)}), f32[16,8,3,128]{3,1,2,0:T(8,128)S(1)}, u32[]{:S(2)}, u32[]{:S(2)}) async-start(f32[16,8,3,128]{3,1,2,0:T(8,128)} %copy.45), calls=%async_computation.2 | async-start | bytes 393216 | tf_op jit(solution)/shard_map/all_to_all | solution.py:96
  138.8 12.5 %all-to-all-start.4 = ((f32[16,8,3,128]{3,1,2,0:T(8,128)}), f32[16,8,3,128]{3,1,2,0:T(8,128)S(1)}, u32[]{:S(2)}, u32[]{:S(2)}) async-start(f32[16,8,3,128]{3,1,2,0:T(8,128)} %copy.57), calls=%async_computation.4 | async-start | bytes 393216 | tf_op jit(solution)/shard_map/all_to_all | solution.py:96
  229.2 11.8 %copy-start.7 = (f32[1,4,3,128]{3,1,2,0:T(4,128)}, f32[1,4,3,128]{3,1,2,0:T(4,128)S(1)}, u32[]{:S(2)}) copy-start(f32[1,4,3,128]{3,1,2,0:T(4,128)S(1)} %copy_add_fusion) | copy-start | bytes 18436
